TPU v7x, 32 devices: a whole 2x2x4 slice. The times are simulated.
32 devices in a mesh: dev: 32 (over z, y, x, core).
Axes of the slice: x: 2, y: 2, z: 4, core: 2. Of those that a mesh axis runs over, the one named last changes fastest.
Arguments:
- tokens: bfloat16 [4608, 1536], P('dev'), may hold values from -6 to 6
- conditioning: bfloat16 [4, 1536], replicated, may hold values from -5 to 5
- text_lengths: int32 [4], replicated, may hold values from 86 to 154, as said below
- modulation_weight: bfloat16 [3072, 9216], P('dev'), may hold values from -0.15625 to 0.15625
- project_weight: bfloat16 [3072, 4608], P('dev'), may hold values from -1 to 1
- merge_weight: bfloat16 [3072, 1536], P('dev'), may hold values from -1.25 to 1.25
- up_weight: bfloat16 [3072, 6144], P('dev'), may hold values from -0.15625 to 0.15625
- down_weight: bfloat16 [12288, 1536], P('dev'), may hold values from -0.078125 to 0.078125
- cotangent: bfloat16 [4608, 1536], P('dev'), may hold values from -6 to 6
Outputs:
- layer_out: bfloat16 [4608, 1536], P('dev')
- tokens_grad: float32 [4608, 1536], P('dev')
- conditioning_grad: float32 [4, 1536], replicated
- modulation_grad: float32 [3072, 9216], P('dev')
- project_grad: float32 [3072, 4608], P('dev')
- merge_grad: float32 [3072, 1536], P('dev')
- up_grad: float32 [3072, 6144], P('dev')
- down_grad: float32 [12288, 1536], P('dev')
Inputs may be any that keep to these rules, and one draw needn't show every extreme that they name: `text_lengths`: the text tokens of all sequences sum to 512, so that the sequences fill the packed rows exactly; one sequence has exactly 154 text tokens.
All inputs are finite; a program needn't handle non-finite values.
Results may differ from a plain program's by a relative error of at most 0.025.
The roundings to bfloat16 on the way count: a program that leaves them out, or rounds other values in their place, can miss the bound.
Values may be sent and summed in bfloat16 or wider, within the bound.
A program may use at most 576 MiB of HBM per device.

v0:
```python
import jax
import jax.numpy as jnp
from jax import lax
from jax.sharding import PartitionSpec as P

HEADS = 24
HDIM = 64
IMG = 1024
REACH = 9
TXT_CAP = 144
HIGHEST_PRECISION = lax.Precision.HIGHEST
EPSILON = 1e-06
CONTRACT_LAST = (((1,), (1,)), ((), ()))
CONTRACT_FIRST = (((0,), (0,)), ((), ()))


def passed_along(x, axis, by):
    length = lax.axis_size(axis)
    pairs = [(i, i + by) for i in range(length) if 0 <= i + by < length]
    return lax.ppermute(x, axis, pairs)


def layer_norm(values):
    mean = jnp.mean(values, axis=-1, keepdims=True)
    centred = values - mean
    variance = jnp.mean(centred * centred, axis=-1, keepdims=True)
    inv_std = lax.rsqrt(variance + EPSILON)
    return (centred * inv_std, inv_std)


def norm_back(grad_normed, normed, inv_std):
    mean_grad = jnp.mean(grad_normed, axis=-1, keepdims=True)
    mean_cross = jnp.mean(grad_normed * normed, axis=-1, keepdims=True)
    return inv_std * (grad_normed - mean_grad - normed * mean_cross)


def sequence_index(positions, starts):
    return jnp.sum((starts[None, :] <= positions[:, None]).astype(jnp.int32), axis=1) - 1


def stream_dot(rows, stacked, layout):
    text_rows, text_valid, slot_of_row, is_text = layout
    half = stacked.shape[0] // 2
    image_part = jnp.dot(rows, stacked[:half], preferred_element_type=jnp.float32)
    text_part = jnp.dot(rows[text_rows], stacked[half:], preferred_element_type=jnp.float32)
    return jnp.where(is_text[:, None], text_part[slot_of_row], image_part)


def stream_rows_back(stacked, grad_low, layout):
    text_rows, text_valid, slot_of_row, is_text = layout
    half = stacked.shape[0] // 2
    image_grad = jnp.where(is_text[:, None], jnp.zeros_like(grad_low), grad_low)
    picked = grad_low[text_rows]
    text_grad = jnp.where(text_valid[:, None], picked, jnp.zeros_like(picked))
    image_back = lax.dot_general(
        image_grad, stacked[:half], CONTRACT_LAST, preferred_element_type=jnp.float32
    )
    text_back = lax.dot_general(
        text_grad, stacked[half:], CONTRACT_LAST, preferred_element_type=jnp.float32
    )
    return jnp.where(is_text[:, None], text_back[slot_of_row], image_back)


def split_streams(rows, is_text):
    zeros = jnp.zeros_like(rows)
    return jnp.concatenate(
        [jnp.where(is_text[:, None], zeros, rows), jnp.where(is_text[:, None], rows, zeros)], axis=1
    )


def term_rows(stacked_rows, grad_low):
    return lax.dot_general(
        stacked_rows, grad_low, CONTRACT_FIRST, preferred_element_type=jnp.float32
    )


def gather_tail(merge_weight, up_weight, down_weight):
    return (
        lax.all_gather(merge_weight, "dev", axis=0, tiled=True),
        lax.all_gather(up_weight, "dev", axis=0, tiled=True),
        lax.all_gather(down_weight, "dev", axis=0, tiled=True),
    )


def heads_last(stacked, count):
    return jnp.transpose(stacked, (1, 0, 2)).reshape(count, HEADS * HDIM)


def on_device(
    tokens,
    conditioning,
    text_lengths,
    modulation_weight,
    project_weight,
    merge_weight,
    up_weight,
    down_weight,
    cotangent,
):
    rows_dev = tokens.shape[0]
    width = tokens.shape[1]
    shard_rows = modulation_weight.shape[0]
    seq_count = conditioning.shape[0]
    devices = lax.axis_size("dev")
    device = lax.axis_index("dev")
    window = (2 * REACH + 1) * rows_dev
    scale = HDIM ** (-0.5)
    own_stream = device * shard_rows // width
    feature_start = device * shard_rows % width
    lengths = IMG + text_lengths
    ends = jnp.cumsum(lengths)
    starts = jnp.concatenate([jnp.zeros((1,), jnp.int32), ends[:-1]])
    positions = device * rows_dev + jnp.arange(rows_dev, dtype=jnp.int32)
    row_seq = sequence_index(positions, starts)
    row_start = jnp.max(
        jnp.where(starts[None, :] <= positions[:, None], starts[None, :], 0), axis=1
    )
    is_text = positions - row_start >= IMG
    text_count = jnp.cumsum(is_text.astype(jnp.int32))
    slot_of_row = jnp.clip(text_count - 1, 0, TXT_CAP - 1)
    slot_range = jnp.arange(TXT_CAP, dtype=jnp.int32)
    text_rows = jnp.clip(
        jnp.sum((text_count[None, :] <= slot_range[:, None]).astype(jnp.int32), axis=1),
        0,
        rows_dev - 1,
    )
    text_valid = slot_range < text_count[-1]
    layout = (text_rows, text_valid, slot_of_row, is_text)
    codes = row_seq * 2 + is_text.astype(jnp.int32)
    one_hot = (codes[:, None] == jnp.arange(2 * seq_count, dtype=jnp.int32)[None, :]).astype(
        jnp.float32
    )
    key_positions = device * rows_dev - REACH * rows_dev + jnp.arange(window, dtype=jnp.int32)
    key_valid = (key_positions >= 0) & (key_positions < devices * rows_dev)
    key_seq = sequence_index(key_positions, starts)
    mask = (row_seq[:, None] == key_seq[None, :]) & key_valid[None, :]
    cond_float = conditioning.astype(jnp.float32)
    silu_low = jax.nn.silu(cond_float).astype(jnp.bfloat16)
    silu_part = lax.dynamic_slice_in_dim(silu_low, feature_start, shard_rows, 1)
    mod_full, project_full = (
        lax.all_gather(modulation_weight, "dev", axis=0, tiled=True),
        lax.all_gather(project_weight, "dev", axis=0, tiled=True),
    )
    mod_table = jnp.einsum(
        "sd,jdc->sjc",
        silu_low,
        mod_full.reshape(2, width, 6 * width),
        preferred_element_type=jnp.float32,
    )
    mod_rows = jnp.dot(
        one_hot,
        mod_table.reshape(2 * seq_count, 6 * width),
        precision=HIGHEST_PRECISION,
        preferred_element_type=jnp.float32,
    )
    shift_a, scale_a, gate_a, shift_b, scale_b, gate_b = jnp.split(mod_rows, 6, axis=1)
    inputs = tokens.astype(jnp.float32)
    normed_a, inv_a = layer_norm(inputs)
    hidden_a = (normed_a * (1.0 + scale_a) + shift_a).astype(jnp.bfloat16)
    projected = stream_dot(hidden_a, project_full, layout).astype(jnp.bfloat16)
    queries, keys, values = jnp.split(projected, 3, axis=1)
    key_pieces = []
    value_pieces = []
    for offset in range(-REACH, REACH + 1):
        if offset == 0:
            key_pieces.append(keys)
            value_pieces.append(values)
        else:
            got_keys, got_values = passed_along((keys, values), "dev", -offset)
            key_pieces.append(got_keys)
            value_pieces.append(got_values)
    window_keys = jnp.concatenate(key_pieces, axis=0)
    window_values = jnp.concatenate(value_pieces, axis=0)

    def head_forward(head):
        query = lax.dynamic_slice_in_dim(queries, head * HDIM, HDIM, 1)
        key_cols = lax.dynamic_slice_in_dim(window_keys, head * HDIM, HDIM, 1)
        value_cols = lax.dynamic_slice_in_dim(window_values, head * HDIM, HDIM, 1)
        scores = (
            lax.dot_general(query, key_cols, CONTRACT_LAST, preferred_element_type=jnp.float32)
            * scale
        )
        masked = jnp.where(mask, scores, -jnp.inf)
        top = jnp.max(masked, axis=1, keepdims=True)
        exponent = jnp.exp(masked - top)
        total = jnp.sum(exponent, axis=1, keepdims=True)
        probs = (exponent / total).astype(jnp.bfloat16)
        attended_head = jnp.dot(probs, value_cols, preferred_element_type=jnp.float32)
        return (attended_head, (top + jnp.log(total))[:, 0])

    head_out, log_totals = lax.map(head_forward, jnp.arange(HEADS, dtype=jnp.int32))
    attended = heads_last(head_out, rows_dev).astype(jnp.bfloat16)
    merge_full, up_full, down_full = gather_tail(merge_weight, up_weight, down_weight)
    merged = stream_dot(attended, merge_full, layout)
    middle = inputs + gate_a * merged
    normed_b, inv_b = layer_norm(middle)
    hidden_b = (normed_b * (1.0 + scale_b) + shift_b).astype(jnp.bfloat16)
    upper = stream_dot(hidden_b, up_full, layout)
    activated = jax.nn.gelu(upper, approximate=True).astype(jnp.bfloat16)
    lowered = stream_dot(activated, down_full, layout)
    layer_out = (middle + gate_b * lowered).astype(jnp.bfloat16)
    grad_out = cotangent.astype(jnp.float32)
    grad_gate_b = grad_out * lowered
    grad_lowered = (gate_b * grad_out).astype(jnp.bfloat16)
    merge_again, up_again, down_again = gather_tail(merge_weight, up_weight, down_weight)
    grad_activated = stream_rows_back(down_again, grad_lowered, layout)
    activated_split = split_streams(activated, is_text)
    down_grad = lax.psum_scatter(
        term_rows(activated_split, grad_lowered), "dev", scatter_dimension=0, tiled=True
    )
    gelu_pull = jax.vjp(lambda value_in: jax.nn.gelu(value_in, approximate=True), upper)[1]
    grad_upper = gelu_pull(grad_activated)[0].astype(jnp.bfloat16)
    grad_hidden_b = stream_rows_back(up_again, grad_upper, layout)
    grad_scale_b = grad_hidden_b * normed_b
    grad_middle = grad_out + norm_back(grad_hidden_b * (1.0 + scale_b), normed_b, inv_b)
    grad_gate_a = grad_middle * merged
    grad_merged = (gate_a * grad_middle).astype(jnp.bfloat16)
    grad_attended = stream_rows_back(merge_again, grad_merged, layout).astype(jnp.bfloat16)
    attended_split = split_streams(attended, is_text)
    hidden_b_split = split_streams(hidden_b, is_text)

    def head_backward(head):
        query = lax.dynamic_slice_in_dim(queries, head * HDIM, HDIM, 1)
        key_cols = lax.dynamic_slice_in_dim(window_keys, head * HDIM, HDIM, 1)
        value_cols = lax.dynamic_slice_in_dim(window_values, head * HDIM, HDIM, 1)
        grad_head = lax.dynamic_slice_in_dim(grad_attended, head * HDIM, HDIM, 1)
        log_total = log_totals[head]
        scores = (
            lax.dot_general(query, key_cols, CONTRACT_LAST, preferred_element_type=jnp.float32)
            * scale
        )
        probs = jnp.where(mask, jnp.exp(scores - log_total[:, None]), 0.0)
        grad_probs = lax.dot_general(
            grad_head, value_cols, CONTRACT_LAST, preferred_element_type=jnp.float32
        )
        inner = jnp.sum(probs * grad_probs, axis=1, keepdims=True)
        grad_scores = (probs * (grad_probs - inner)).astype(jnp.bfloat16)
        grad_query = jnp.dot(grad_scores, key_cols, preferred_element_type=jnp.float32) * scale
        grad_key = (
            lax.dot_general(grad_scores, query, CONTRACT_FIRST, preferred_element_type=jnp.float32)
            * scale
        )
        grad_value = lax.dot_general(
            probs.astype(jnp.bfloat16),
            grad_head,
            CONTRACT_FIRST,
            preferred_element_type=jnp.float32,
        )
        return (grad_query, grad_key, grad_value)

    head_queries, head_keys, head_values = lax.map(
        head_backward, jnp.arange(HEADS, dtype=jnp.int32)
    )
    grad_queries = heads_last(head_queries, rows_dev)
    grad_keys = heads_last(head_keys, window)
    grad_values = heads_last(head_values, window)
    centre = REACH * rows_dev
    key_total = grad_keys[centre : centre + rows_dev]
    value_total = grad_values[centre : centre + rows_dev]
    for offset in range(-REACH, REACH + 1):
        if offset != 0:
            block = (offset + REACH) * rows_dev
            got_key, got_value = (
                passed_along(
                    grad_keys[block : block + rows_dev].astype(jnp.bfloat16), "dev", offset
                ).astype(jnp.float32),
                passed_along(
                    grad_values[block : block + rows_dev].astype(jnp.bfloat16), "dev", offset
                ).astype(jnp.float32),
            )
            key_total = key_total + got_key
            value_total = value_total + got_value
    grad_projected = jnp.concatenate([grad_queries, key_total, value_total], axis=1).astype(
        jnp.bfloat16
    )
    project_again = lax.all_gather(project_weight, "dev", axis=0, tiled=True)
    grad_hidden_a = stream_rows_back(project_again, grad_projected, layout)
    hidden_a_split = split_streams(hidden_a, is_text)
    summed = lax.psum_scatter(
        jnp.concatenate(
            [
                term_rows(attended_split, grad_merged),
                term_rows(hidden_b_split, grad_upper),
                term_rows(hidden_a_split, grad_projected),
            ],
            axis=1,
        ),
        "dev",
        scatter_dimension=0,
        tiled=True,
    )
    merge_grad = summed[:, :width]
    up_grad = summed[:, width : width + up_weight.shape[1]]
    project_grad = summed[:, width + up_weight.shape[1] :]
    grad_scale_a = grad_hidden_a * normed_a
    tokens_grad = grad_middle + norm_back(grad_hidden_a * (1.0 + scale_a), normed_a, inv_a)
    grad_mod_rows = jnp.concatenate(
        [grad_hidden_a, grad_scale_a, grad_gate_a, grad_hidden_b, grad_scale_b, grad_gate_b], axis=1
    )
    local_table = lax.dot_general(
        one_hot,
        grad_mod_rows,
        CONTRACT_FIRST,
        precision=HIGHEST_PRECISION,
        preferred_element_type=jnp.float32,
    )
    grad_table = lax.psum(local_table.reshape(seq_count, 2, 6 * width), "dev").astype(jnp.bfloat16)
    own_grads = lax.dynamic_index_in_dim(grad_table, own_stream, 1, keepdims=False)
    modulation_grad = lax.dot_general(
        silu_part, own_grads, CONTRACT_FIRST, preferred_element_type=jnp.float32
    )
    grad_piece = lax.dot_general(
        own_grads, modulation_weight, CONTRACT_LAST, preferred_element_type=jnp.float32
    )
    gathered = lax.all_gather(grad_piece, "dev", axis=1, tiled=True)
    grad_silu = gathered[:, :width] + gathered[:, width:]
    silu_pull = jax.vjp(jax.nn.silu, cond_float)[1]
    conditioning_grad = silu_pull(grad_silu)[0]
    return (
        layer_out,
        tokens_grad,
        conditioning_grad,
        modulation_grad,
        project_grad,
        merge_grad,
        up_grad,
        down_grad,
    )


def solution(mesh):
    return jax.shard_map(
        on_device,
        mesh=mesh,
        in_specs=(
            P("dev", None),
            P(),
            P(),
            P("dev", None),
            P("dev", None),
            P("dev", None),
            P("dev", None),
            P("dev", None),
            P("dev", None),
        ),
        out_specs=(
            P("dev", None),
            P("dev", None),
            P(),
            P("dev", None),
            P("dev", None),
            P("dev", None),
            P("dev", None),
            P("dev", None),
        ),
        check_vma=False,
    )
```

profile of v0, /device:TPU:0, one launch (start us, length us, event | category | flops | bytes accessed | tf_op | source)
XLA Modules:
  0.0 4166.2 jit_solution(7847232623532628059)
XLA Ops:
  13.0 306.8 %all-gather.7.cloned.1.call-done = bf16[3072,9216]{1,0:T(8,128)(2,1)} async-done(((bf16[96,9216]{1,0:T(8,128)(2,1)}), bf16[3072,9216]{1,0:T(8,128)(2,1)}) %all-gather.7.cloned.1.call-update) | async-done | bytes 56623120 | tf_op jit(solution)/shard_map/all_gather | solution.py:141
  319.7 20.9 fusion.179
  347.9 142.7 %all-gather.9.cloned.1.call-done = bf16[3072,4608]{1,0:T(8,128)(2,1)} async-done(((bf16[96,4608]{1,0:T(8,128)(2,1)}), bf16[3072,4608]{1,0:T(8,128)(2,1)}) %all-gather.9.cloned.1.call-update) | async-done | bytes 28311568 | tf_op jit(solution)/shard_map/all_gather | solution.py:142
  526.7 14.3 collective-permute-done.18
  555.9 16.0 collective-permute-start.4
  579.8 11.5 collective-permute-start.5
  591.4 12.9 collective-permute-start.6
  624.0 25.8 collective-permute-start.19
  649.9 26.3 collective-permute-start.20
  676.2 20.0 collective-permute-start.21
  697.7 18.0 collective-permute-done.21
  715.7 21.0 collective-permute-start.23
  748.6 15.8 collective-permute-start.26
  781.4 66.0 %collective-permute-done.29 = bf16[144,1536]{1,0:T(8,128)(2,1)S(1)} collective-permute-done((bf16[144,1536]{1,0:T(8,128)(2,1)S(1)}, bf16[144,1536]{1,0:T(8,128)(2,1)S(1)}, u32[]{:S(2)}, u32[]{:S(2)}) %collective-permute-start.29) | collective-permute-done | bytes 442400 | tf_op jit(solution)/shard_map/ppermute | solution.py:20
  848.8 9.3 collective-permute-done.30
  859.3 27.8 collective-permute-done.31
  888.4 10.1 collective-permute-done.32
  906.2 65.4 %collective-permute-done.10 = bf16[144,1536]{1,0:T(8,128)(2,1)S(1)} collective-permute-done((bf16[144,1536]{1,0:T(8,128)(2,1)S(1)}, bf16[144,1536]{1,0:T(8,128)(2,1)S(1)}, u32[]{:S(2)}, u32[]{:S(2)}) %collective-permute-start.10) | collective-permute-done | bytes 442400 | tf_op jit(solution)/shard_map/ppermute | solution.py:20
  983.1 58.3 %collective-permute-done.13 = bf16[144,1536]{1,0:T(8,128)(2,1)S(1)} collective-permute-done((bf16[144,1536]{1,0:T(8,128)(2,1)S(1)}, bf16[144,1536]{1,0:T(8,128)(2,1)S(1)}, u32[]{:S(2)}, u32[]{:S(2)}) %collective-permute-start.13) | collective-permute-done | bytes 442400 | tf_op jit(solution)/shard_map/ppermute | solution.py:20
  1041.5 19.6 collective-permute-done.14
  1064.5 164.2 %while.28 = (s32[]{:T(128)}, bf16[24,144,64]{1,2,0:T(8,128)(2,1)S(1)}, f32[24,144]{1,0:T(8,128)}, s32[24]{0:T(128)S(1)}, bf16[144,1536]{1,0:T(8,128)(2,1)S(1)}, ...) while((s32[]{:T(128)}, ...), condition=%wide.region_12.13_spmd.clone, body=%wide.region_9.12_spmd.clone.sunk | while | flops 104799600 | bytes 6301395 | solution.py:191
  1259.3 10.3 fusion.39
  1273.0 11.5 broadcast_select_fusion.1
  1284.6 12.7 fusion.85
  1300.1 14.2 fusion.47
  1317.8 12.6 fusion.199
  1334.3 10.7 fusion.41
  1348.4 11.1 multiply_convert_fusion.2
  1372.0 332.8 %while.29 = (s32[]{:T(128)}, bf16[24,144,64]{1,2,0:T(8,128)(2,1)S(1)}, f32[24,2736,64]{1,2,0:T(8,128)}, f32[24,2736,64]{1,2,0:T(8,128)}, s32[24]{0:T(128)S(1)}, ...) while((s32[]{:T(128)}, ...), condition=%wide.region_19.20_spmd.clone, body=%wide.region_17.19_spmd.clone.sunk | while | flops 256667760 | bytes 15618069 | solution.py:251
  1712.1 9.2 fusion.207
  1740.0 16.1 collective-permute-done.55
  1768.7 14.0 collective-permute-done.57
  1798.8 20.5 collective-permute-start.65
  1853.0 16.7 collective-permute-start.68
  1873.8 13.4 fusion.206
  1929.5 28.2 fusion.139
  1983.6 10.9 collective-permute-start.45
  1994.6 18.1 collective-permute-start.46
  2020.9 9.3 fusion.135
  2042.0 9.5 collective-permute-start.53
  2068.0 20.6 fusion.143
  2088.6 97.4 %pad_maximum_fusion = f32[3072,12288]{1,0:T(8,128)} fusion(f32[3072,4608]{1,0:T(8,128)} %fusion.143, f32[3072,6144]{1,0:T(8,128)} %fusion.139, f32[3072,1536]{1,0:T(8,128)} %fusion.135), kind=kLoop, calls=%fused_computation.61 | loop fusion | flops 75497472 | bytes 301989888 | tf_op jit(solution)/shard_map/concatenate | solution.py:280
  2188.9 29.0 fusion.86
  2231.5 9.7 fusion.200
  2254.2 105.1 %all-reduce.2 = bf16[4,2,9216]{2,0,1:T(4,128)(2,1)S(1)} all-reduce(f32[4,2,9216]{2,0,1:T(4,128)S(1)} %copy.187), channel_id=1, replica_groups=mesh['dev'=32] {'dev'}, use_global_device_ids=true, to_apply=%region_22.23 | all-reduce | flops 73728 | bytes 442368 | tf_op jit(solution)/shard_map/psum | solution.py:307
  2359.9 39.6 all-gather
  2402.8 1092.8 %reduce-scatter.3.cloned.1.call-done = f32[96,12288]{1,0:T(8,128)} async-done(((f32[3072,12288]{1,0:T(8,128)}), f32[96,12288]{1,0:T(8,128)}) %reduce-scatter.3.cloned.1.call-update) | async-done | bytes 4718608 | tf_op jit(solution)/shard_map/reduce_scatter | solution.py:279
  3503.5 655.4 %reduce-scatter.5.cloned.1.call-done = f32[384,1536]{1,0:T(8,128)} async-done(((f32[12288,1536]{1,0:T(8,128)}), f32[384,1536]{1,0:T(8,128)}) %reduce-scatter.5.cloned.1.call-update) | async-done | bytes 2359312 | tf_op jit(solution)/shard_map/reduce_scatter | solution.py:208
  (800 shorter events, 864.2 us)
Async XLA Ops:
  7.2 312.5 %all-gather.7.cloned.1.call-start = ((), (), s32[]{:S(2)}) async-start(), calls=%async_computation.2 | async-start | bytes 58392576 | tf_op jit(solution)/shard_map/all_gather | solution.py:141
  7.9 482.6 %all-gather.9.cloned.1.call-start = ((), (), s32[]{:S(2)}) async-start(), calls=%async_computation.3 | async-start | bytes 29196288 | tf_op jit(solution)/shard_map/all_gather | solution.py:142
  8.7 1222.1 %all-gather.11.cloned.1.call-start = ((), (), s32[]{:S(2)}) async-start(), calls=%async_computation.4 | async-start | bytes 9732096 | tf_op jit(solution)/shard_map/all_gather | solution.py:79
  9.4 1238.4 %all-gather.13.cloned.1.call-start = ((), (), s32[]{:S(2)}) async-start(), calls=%async_computation.5 | async-start | bytes 38928384 | tf_op jit(solution)/shard_map/all_gather | solution.py:80
  10.0 1249.3 %all-gather.15.cloned.1.call-start = ((), (), s32[]{:S(2)}) async-start(), calls=%async_computation.6 | async-start | bytes 38928384 | tf_op jit(solution)/shard_map/all_gather | solution.py:81
  10.6 3485.0 %reduce-scatter.3.cloned.1.call-start = ((), (), s32[]{:S(2)}) async-start(), calls=%async_computation.7 | async-start | bytes 155713536 | tf_op jit(solution)/shard_map/reduce_scatter | solution.py:279
  516.3 386.2 %collective-permute-start.35 = (bf16[144,1536]{1,0:T(8,128)(2,1)S(1)}, bf16[144,1536]{1,0:T(8,128)(2,1)S(1)}, u32[]{:S(2)}, u32[]{:S(2)}) collective-permute-start(bf16[144,1536]{1,0:T(8,128)(2,1)S(1)} %get-tuple-element.282), channel_id=1, source_target_pairs={{9,0},{10,1},{11,2},{12,3},{13,4},{14,5},{15,6},{16,7},{17,8},{18,... | collective-permute-start | bytes 1327112 | tf_op jit(solution)/shard_map/ppermute | solution.py:20
  517.6 383.6 %collective-permute-start.34 = (bf16[144,1536]{1,0:T(8,128)(2,1)S(1)}, bf16[144,1536]{1,0:T(8,128)(2,1)S(1)}, u32[]{:S(2)}, u32[]{:S(2)}) collective-permute-start(bf16[144,1536]{1,0:T(8,128)(2,1)S(1)} %get-tuple-element.282), channel_id=1, source_target_pairs={{8,0},{9,1},{10,2},{11,3},{12,4},{13,5},{14,6},{15,7},{16,8},{17,9... | collective-permute-start | bytes 1327112 | tf_op jit(solution)/shard_map/ppermute | solution.py:20
  518.9 380.9 %collective-permute-start.33 = (bf16[144,1536]{1,0:T(8,128)(2,1)S(1)}, bf16[144,1536]{1,0:T(8,128)(2,1)S(1)}, u32[]{:S(2)}, u32[]{:S(2)}) collective-permute-start(bf16[144,1536]{1,0:T(8,128)(2,1)S(1)} %get-tuple-element.282), channel_id=1, source_target_pairs={{7,0},{8,1},{9,2},{10,3},{11,4},{12,5},{13,6},{14,7},{15,8},{16,9}... | collective-permute-start | bytes 1327112 | tf_op jit(solution)/shard_map/ppermute | solution.py:20
  555.9 35.5 collective-permute-start.4
  612.4 37.5 collective-permute-start.8
  624.0 52.2 %collective-permute-start.19 = (bf16[144,1536]{1,0:T(8,128)(2,1)S(1)}, bf16[144,1536]{1,0:T(8,128)(2,1)S(1)}, u32[]{:S(2)}, u32[]{:S(2)}) collective-permute-start(bf16[144,1536]{1,0:T(8,128)(2,1)S(1)} %get-tuple-element.282), channel_id=1, source_target_pairs={{0,8},{1,9},{2,10},{3,11},{4,12},{5,13},{6,14},{7,15},{8,16},{9,17... | collective-permute-start | bytes 1327112 | tf_op jit(solution)/shard_map/ppermute | solution.py:20
  649.9 46.4 %collective-permute-start.20 = (bf16[144,1536]{1,0:T(8,128)(2,1)S(1)}, bf16[144,1536]{1,0:T(8,128)(2,1)S(1)}, u32[]{:S(2)}, u32[]{:S(2)}) collective-permute-start(bf16[144,1536]{1,0:T(8,128)(2,1)S(1)} %get-tuple-element.282), channel_id=1, source_target_pairs={{0,7},{1,8},{2,9},{3,10},{4,11},{5,12},{6,13},{7,14},{8,15},{9,16}... | collective-permute-start | bytes 1327112 | tf_op jit(solution)/shard_map/ppermute | solution.py:20
  676.2 39.5 collective-permute-start.21
  696.3 40.5 collective-permute-start.22
  773.8 73.6 %collective-permute-start.29 = (bf16[144,1536]{1,0:T(8,128)(2,1)S(1)}, bf16[144,1536]{1,0:T(8,128)(2,1)S(1)}, u32[]{:S(2)}, u32[]{:S(2)}) collective-permute-start(bf16[144,1536]{1,0:T(8,128)(2,1)S(1)} %get-tuple-element.282), channel_id=1, source_target_pairs={{3,0},{4,1},{5,2},{6,3},{7,4},{8,5},{9,6},{10,7},{11,8},{12,9},{13... | collective-permute-start | bytes 1327112 | tf_op jit(solution)/shard_map/ppermute | solution.py:20
  780.1 77.9 %collective-permute-start.30 = (bf16[144,1536]{1,0:T(8,128)(2,1)S(1)}, bf16[144,1536]{1,0:T(8,128)(2,1)S(1)}, u32[]{:S(2)}, u32[]{:S(2)}) collective-permute-start(bf16[144,1536]{1,0:T(8,128)(2,1)S(1)} %get-tuple-element.282), channel_id=1, source_target_pairs={{4,0},{5,1},{6,2},{7,3},{8,4},{9,5},{10,6},{11,7},{12,8},{13,9},{1... | collective-permute-start | bytes 1327112 | tf_op jit(solution)/shard_map/ppermute | solution.py:20
  847.4 39.7 collective-permute-start.31
  858.0 40.5 collective-permute-start.32
  887.1 174.1 %collective-permute-start.17 = (bf16[144,1536]{1,0:T(8,128)(2,1)S(1)}, bf16[144,1536]{1,0:T(8,128)(2,1)S(1)}, u32[]{:S(2)}, u32[]{:S(2)}) collective-permute-start(bf16[144,1536]{1,0:T(8,128)(2,1)S(1)} %get-tuple-element.283), channel_id=1, source_target_pairs={{9,0},{10,1},{11,2},{12,3},{13,4},{14,5},{15,6},{16,7},{17,8},{18,... | collective-permute-start | bytes 1327112 | tf_op jit(solution)/shard_map/ppermute | solution.py:20
  898.5 162.6 %collective-permute-start.16 = (bf16[144,1536]{1,0:T(8,128)(2,1)S(1)}, bf16[144,1536]{1,0:T(8,128)(2,1)S(1)}, u32[]{:S(2)}, u32[]{:S(2)}) collective-permute-start(bf16[144,1536]{1,0:T(8,128)(2,1)S(1)} %get-tuple-element.283), channel_id=1, source_target_pairs={{8,0},{9,1},{10,2},{11,3},{12,4},{13,5},{14,6},{15,7},{16,8},{17,9... | collective-permute-start | bytes 1327112 | tf_op jit(solution)/shard_map/ppermute | solution.py:20
  899.8 161.2 %collective-permute-start.15 = (bf16[144,1536]{1,0:T(8,128)(2,1)S(1)}, bf16[144,1536]{1,0:T(8,128)(2,1)S(1)}, u32[]{:S(2)}, u32[]{:S(2)}) collective-permute-start(bf16[144,1536]{1,0:T(8,128)(2,1)S(1)} %get-tuple-element.283), channel_id=1, source_target_pairs={{7,0},{8,1},{9,2},{10,3},{11,4},{12,5},{13,6},{14,7},{15,8},{16,9}... | collective-permute-start | bytes 1327112 | tf_op jit(solution)/shard_map/ppermute | solution.py:20
  902.5 69.1 %collective-permute-start.10 = (bf16[144,1536]{1,0:T(8,128)(2,1)S(1)}, bf16[144,1536]{1,0:T(8,128)(2,1)S(1)}, u32[]{:S(2)}, u32[]{:S(2)}) collective-permute-start(bf16[144,1536]{1,0:T(8,128)(2,1)S(1)} %get-tuple-element.283), channel_id=1, source_target_pairs={{2,0},{3,1},{4,2},{5,3},{6,4},{7,5},{8,6},{9,7},{10,8},{11,9},{12,... | collective-permute-start | bytes 1327112 | tf_op jit(solution)/shard_map/ppermute | solution.py:20
  904.9 70.3 %collective-permute-start.11 = (bf16[144,1536]{1,0:T(8,128)(2,1)S(1)}, bf16[144,1536]{1,0:T(8,128)(2,1)S(1)}, u32[]{:S(2)}, u32[]{:S(2)}) collective-permute-start(bf16[144,1536]{1,0:T(8,128)(2,1)S(1)} %get-tuple-element.283), channel_id=1, source_target_pairs={{3,0},{4,1},{5,2},{6,3},{7,4},{8,5},{9,6},{10,7},{11,8},{12,9},{13... | collective-permute-start | bytes 1327112 | tf_op jit(solution)/shard_map/ppermute | solution.py:20
  975.2 66.3 %collective-permute-start.13 = (bf16[144,1536]{1,0:T(8,128)(2,1)S(1)}, bf16[144,1536]{1,0:T(8,128)(2,1)S(1)}, u32[]{:S(2)}, u32[]{:S(2)}) collective-permute-start(bf16[144,1536]{1,0:T(8,128)(2,1)S(1)} %get-tuple-element.283), channel_id=1, source_target_pairs={{5,0},{6,1},{7,2},{8,3},{9,4},{10,5},{11,6},{12,7},{13,8},{14,9},{... | collective-permute-start | bytes 1327112 | tf_op jit(solution)/shard_map/ppermute | solution.py:20
  981.8 79.2 %collective-permute-start.14 = (bf16[144,1536]{1,0:T(8,128)(2,1)S(1)}, bf16[144,1536]{1,0:T(8,128)(2,1)S(1)}, u32[]{:S(2)}, u32[]{:S(2)}) collective-permute-start(bf16[144,1536]{1,0:T(8,128)(2,1)S(1)} %get-tuple-element.283), channel_id=1, source_target_pairs={{6,0},{7,1},{8,2},{9,3},{10,4},{11,5},{12,6},{13,7},{14,8},{15,9},... | collective-permute-start | bytes 1327112 | tf_op jit(solution)/shard_map/ppermute | solution.py:20
  1734.0 48.8 %collective-permute-start.57 = (bf16[144,1536]{1,0:T(8,128)(2,1)}, bf16[144,1536]{1,0:T(8,128)(2,1)}, u32[]{:S(2)}, u32[]{:S(2)}) collective-permute-start(bf16[144,1536]{1,0:T(8,128)(2,1)} %copy.216), channel_id=1, source_target_pairs={{6,0},{7,1},{8,2},{9,3},{10,4},{11,5},{12,6},{13,7},{14,8},{15,9},... | collective-permute-start | bytes 1327112 | tf_op jit(solution)/shard_map/ppermute | solution.py:20
  1735.3 48.8 %collective-permute-start.58 = (bf16[144,1536]{1,0:T(8,128)(2,1)}, bf16[144,1536]{1,0:T(8,128)(2,1)}, u32[]{:S(2)}, u32[]{:S(2)}) collective-permute-start(bf16[144,1536]{1,0:T(8,128)(2,1)} %copy.217), channel_id=1, source_target_pairs={{5,0},{6,1},{7,2},{8,3},{9,4},{10,5},{11,6},{12,7},{13,8},{14,9},{... | collective-permute-start | bytes 1327112 | tf_op jit(solution)/shard_map/ppermute | solution.py:20
  1738.7 52.7 %collective-permute-start.59 = (bf16[144,1536]{1,0:T(8,128)(2,1)}, bf16[144,1536]{1,0:T(8,128)(2,1)}, u32[]{:S(2)}, u32[]{:S(2)}) collective-permute-start(bf16[144,1536]{1,0:T(8,128)(2,1)} %copy.218), channel_id=1, source_target_pairs={{4,0},{5,1},{6,2},{7,3},{8,4},{9,5},{10,6},{11,7},{12,8},{13,9},{1... | collective-permute-start | bytes 1327112 | tf_op jit(solution)/shard_map/ppermute | solution.py:20
  1756.2 42.6 %collective-permute-start.60 = (bf16[144,1536]{1,0:T(8,128)(2,1)}, bf16[144,1536]{1,0:T(8,128)(2,1)}, u32[]{:S(2)}, u32[]{:S(2)}) collective-permute-start(bf16[144,1536]{1,0:T(8,128)(2,1)} %copy.219), channel_id=1, source_target_pairs={{3,0},{4,1},{5,2},{6,3},{7,4},{8,5},{9,6},{10,7},{11,8},{12,9},{13... | collective-permute-start | bytes 1327112 | tf_op jit(solution)/shard_map/ppermute | solution.py:20
  1767.4 74.9 %collective-permute-start.61 = (bf16[144,1536]{1,0:T(8,128)(2,1)}, bf16[144,1536]{1,0:T(8,128)(2,1)}, u32[]{:S(2)}, u32[]{:S(2)}) collective-permute-start(bf16[144,1536]{1,0:T(8,128)(2,1)} %copy.220), channel_id=1, source_target_pairs={{2,0},{3,1},{4,2},{5,3},{6,4},{7,5},{8,6},{9,7},{10,8},{11,9},{12,... | collective-permute-start | bytes 1327112 | tf_op jit(solution)/shard_map/ppermute | solution.py:20
  1782.7 66.8 %collective-permute-start.62 = (bf16[144,1536]{1,0:T(8,128)(2,1)}, bf16[144,1536]{1,0:T(8,128)(2,1)}, u32[]{:S(2)}, u32[]{:S(2)}) collective-permute-start(bf16[144,1536]{1,0:T(8,128)(2,1)} %copy.221), channel_id=1, source_target_pairs={{1,0},{2,1},{3,2},{4,3},{5,4},{6,5},{7,6},{8,7},{9,8},{10,9},{11,1... | collective-permute-start | bytes 1327112 | tf_op jit(solution)/shard_map/ppermute | solution.py:20
  1784.0 68.9 %collective-permute-start.63 = (bf16[144,1536]{1,0:T(8,128)(2,1)}, bf16[144,1536]{1,0:T(8,128)(2,1)}, u32[]{:S(2)}, u32[]{:S(2)}) collective-permute-start(bf16[144,1536]{1,0:T(8,128)(2,1)} %copy.222), channel_id=1, source_target_pairs={{0,1},{1,2},{2,3},{3,4},{4,5},{5,6},{6,7},{7,8},{8,9},{9,10},{10,1... | collective-permute-start | bytes 1327112 | tf_op jit(solution)/shard_map/ppermute | solution.py:20
  1791.5 78.2 %collective-permute-start.64 = (bf16[144,1536]{1,0:T(8,128)(2,1)}, bf16[144,1536]{1,0:T(8,128)(2,1)}, u32[]{:S(2)}, u32[]{:S(2)}) collective-permute-start(bf16[144,1536]{1,0:T(8,128)(2,1)} %copy.223), channel_id=1, source_target_pairs={{0,2},{1,3},{2,4},{3,5},{4,6},{5,7},{6,8},{7,9},{8,10},{9,11},{10,... | collective-permute-start | bytes 1327112 | tf_op jit(solution)/shard_map/ppermute | solution.py:20
  1798.8 73.0 %collective-permute-start.65 = (bf16[144,1536]{1,0:T(8,128)(2,1)S(1)}, bf16[144,1536]{1,0:T(8,128)(2,1)}, u32[]{:S(2)}, u32[]{:S(2)}) collective-permute-start(bf16[144,1536]{1,0:T(8,128)(2,1)S(1)} %copy.224), channel_id=1, source_target_pairs={{0,3},{1,4},{2,5},{3,6},{4,7},{5,8},{6,9},{7,10},{8,11},{9,12},{10... | collective-permute-start | bytes 1327112 | tf_op jit(solution)/shard_map/ppermute | solution.py:20
  1842.3 61.1 %collective-permute-start.66 = (bf16[144,1536]{1,0:T(8,128)(2,1)}, bf16[144,1536]{1,0:T(8,128)(2,1)}, u32[]{:S(2)}, u32[]{:S(2)}) collective-permute-start(bf16[144,1536]{1,0:T(8,128)(2,1)} %copy.225), channel_id=1, source_target_pairs={{0,4},{1,5},{2,6},{3,7},{4,8},{5,9},{6,10},{7,11},{8,12},{9,13},{1... | collective-permute-start | bytes 1327112 | tf_op jit(solution)/shard_map/ppermute | solution.py:20
  1849.6 55.1 %collective-permute-start.67 = (bf16[144,1536]{1,0:T(8,128)(2,1)}, bf16[144,1536]{1,0:T(8,128)(2,1)}, u32[]{:S(2)}, u32[]{:S(2)}) collective-permute-start(bf16[144,1536]{1,0:T(8,128)(2,1)} %copy.226), channel_id=1, source_target_pairs={{0,5},{1,6},{2,7},{3,8},{4,9},{5,10},{6,11},{7,12},{8,13},{9,14},{... | collective-permute-start | bytes 1327112 | tf_op jit(solution)/shard_map/ppermute | solution.py:20
  1853.0 53.0 %collective-permute-start.68 = (bf16[144,1536]{1,0:T(8,128)(2,1)}, bf16[144,1536]{1,0:T(8,128)(2,1)}, u32[]{:S(2)}, u32[]{:S(2)}) collective-permute-start(bf16[144,1536]{1,0:T(8,128)(2,1)} %copy.227), channel_id=1, source_target_pairs={{0,6},{1,7},{2,8},{3,9},{4,10},{5,11},{6,12},{7,13},{8,14},{9,15},... | collective-permute-start | bytes 1327112 | tf_op jit(solution)/shard_map/ppermute | solution.py:20
  1869.7 37.7 collective-permute-start.69
  1871.7 36.9 collective-permute-start.70
  1914.7 68.9 %collective-permute-start.40 = (bf16[144,1536]{1,0:T(8,128)(2,1)}, bf16[144,1536]{1,0:T(8,128)(2,1)}, u32[]{:S(2)}, u32[]{:S(2)}) collective-permute-start(bf16[144,1536]{1,0:T(8,128)(2,1)} %copy.198), channel_id=1, source_target_pairs={{5,0},{6,1},{7,2},{8,3},{9,4},{10,5},{11,6},{12,7},{13,8},{14,9},{... | collective-permute-start | bytes 1327112 | tf_op jit(solution)/shard_map/ppermute | solution.py:20
  1922.2 72.4 %collective-permute-start.41 = (bf16[144,1536]{1,0:T(8,128)(2,1)}, bf16[144,1536]{1,0:T(8,128)(2,1)}, u32[]{:S(2)}, u32[]{:S(2)}) collective-permute-start(bf16[144,1536]{1,0:T(8,128)(2,1)} %copy.199), channel_id=1, source_target_pairs={{4,0},{5,1},{6,2},{7,3},{8,4},{9,5},{10,6},{11,7},{12,8},{13,9},{1... | collective-permute-start | bytes 1327112 | tf_op jit(solution)/shard_map/ppermute | solution.py:20
  1925.5 87.1 %collective-permute-start.42 = (bf16[144,1536]{1,0:T(8,128)(2,1)}, bf16[144,1536]{1,0:T(8,128)(2,1)}, u32[]{:S(2)}, u32[]{:S(2)}) collective-permute-start(bf16[144,1536]{1,0:T(8,128)(2,1)} %copy.200), channel_id=1, source_target_pairs={{3,0},{4,1},{5,2},{6,3},{7,4},{8,5},{9,6},{10,7},{11,8},{12,9},{13... | collective-permute-start | bytes 1327112 | tf_op jit(solution)/shard_map/ppermute | solution.py:20
  1926.8 90.0 %collective-permute-start.43 = (bf16[144,1536]{1,0:T(8,128)(2,1)}, bf16[144,1536]{1,0:T(8,128)(2,1)}, u32[]{:S(2)}, u32[]{:S(2)}) collective-permute-start(bf16[144,1536]{1,0:T(8,128)(2,1)} %copy.201), channel_id=1, source_target_pairs={{2,0},{3,1},{4,2},{5,3},{6,4},{7,5},{8,6},{9,7},{10,8},{11,9},{12,... | collective-permute-start | bytes 1327112 | tf_op jit(solution)/shard_map/ppermute | solution.py:20
  1928.1 91.4 %collective-permute-start.44 = (bf16[144,1536]{1,0:T(8,128)(2,1)}, bf16[144,1536]{1,0:T(8,128)(2,1)}, u32[]{:S(2)}, u32[]{:S(2)}) collective-permute-start(bf16[144,1536]{1,0:T(8,128)(2,1)} %copy.202), channel_id=1, source_target_pairs={{1,0},{2,1},{3,2},{4,3},{5,4},{6,5},{7,6},{8,7},{9,8},{10,9},{11,1... | collective-permute-start | bytes 1327112 | tf_op jit(solution)/shard_map/ppermute | solution.py:20
  1983.6 46.7 %collective-permute-start.45 = (bf16[144,1536]{1,0:T(8,128)(2,1)}, bf16[144,1536]{1,0:T(8,128)(2,1)S(1)}, u32[]{:S(2)}, u32[]{:S(2)}) collective-permute-start(bf16[144,1536]{1,0:T(8,128)(2,1)} %copy.203), channel_id=1, source_target_pairs={{0,1},{1,2},{2,3},{3,4},{4,5},{5,6},{6,7},{7,8},{8,9},{9,10},{10,1... | collective-permute-start | bytes 1327112 | tf_op jit(solution)/shard_map/ppermute | solution.py:20
  1994.6 38.9 collective-permute-start.46
  2186.0 1972.8 %reduce-scatter.5.cloned.1.call-start = ((), (), s32[]{:S(2)}) async-start(), calls=%async_computation.8 | async-start | bytes 77856768 | tf_op jit(solution)/shard_map/reduce_scatter | solution.py:208
  (107 other events, 7857.7 us)
Sparse Core Ops, SparseCore 0:
  10.9 308.7 all-gather.6
  322.6 167.8 all-gather.8
  493.4 105.1 all-gather.10
  601.4 330.3 all-gather.12
  934.6 275.7 all-gather.14
  2186.2 1309.3 reduce-scatter.2
  3503.7 655.1 reduce-scatter.4
where the time goes:
time: 4190 us; the launch traced here: 4170 us
  waiting for transfers between devices  2590 us (62%)
  matrix products  586 us (14%)
  starting transfers between devices  366 us (9%)
  local copies, waits for them, and re-layouts  237 us (6%)
  other arithmetic  152 us (4%)
  blocking collectives  145 us (3%)
  loops' own time  78.1 us (2%)
    reduce_scatter x1, waiting for transfers between devices, on_device(): lax.psum_scatter(jnp.concatenate([term_rows(attended_split, grad_merged),...  1090 us
    reduce_scatter x1, waiting for transfers between devices, on_device(): lax.psum_scatter(term_rows(activated_split, grad_lowered), 'dev', scatter...  655 us
    ppermute x72, waiting for transfers between devices, passed_along(): return lax.ppermute(x, axis, pairs)  385 us
    ppermute x72, starting transfers between devices, passed_along(): return lax.ppermute(x, axis, pairs)  365 us
    all_gather x1, waiting for transfers between devices, on_device(): lax.all_gather(modulation_weight, 'dev', axis=0, tiled=True)  307 us
    all_gather x1, waiting for transfers between devices, on_device(): lax.all_gather(project_weight, 'dev', axis=0, tiled=True)  143 us
    psum x1, blocking collectives, on_device(): lax.psum(local_table.reshape(seq_count, 2, 6 * width), 'dev')  105 us
    concatenate x1, other arithmetic, on_device(): jnp.concatenate([term_rows(attended_split, grad_merged), term_rows(hidden...  97.4 us
  transfers between devices with their start and end apart: 79, of which 31 were waited for; matrix products, arithmetic and copies ran while one was open for 11% of the time, Pallas kernels for 0%

commit v1 on v0

--- a/solution.py
+++ b/solution.py
@@ -1,7 +1,9 @@
+import functools
 import jax
 import jax.numpy as jnp
 from jax import lax
 from jax.sharding import PartitionSpec as P
+from jax.lax import axis_index, ppermute, psum
 
 HEADS = 24
 HDIM = 64
@@ -12,6 +14,30 @@
 EPSILON = 1e-06
 CONTRACT_LAST = (((1,), (1,)), ((), ()))
 CONTRACT_FIRST = (((0,), (0,)), ((), ()))
+
+
+def wait_racks_all(s0, dim_no):
+    x_next = psum(1, "dev")
+    work_now = axis_index("dev")
+    field_out, y1, carry_in = (x_next, work_now, s0.shape[dim_no])
+    back, r_now = (s0, 1)
+    while r_now < field_out:
+        back = jnp.concatenate(
+            [
+                back,
+                ppermute(
+                    back,
+                    "dev",
+                    list(map(lambda i0: (i0, (i0 - r_now) % field_out), range(field_out))),
+                ),
+            ],
+            dim_no,
+        )
+        r_now = 2 * r_now
+    return jnp.roll(back, y1 * carry_in, dim_no)
+
+
+touch_tokens = functools.partial(wait_racks_all, dim_no=0)
 
 
 def passed_along(x, axis, by):
@@ -139,7 +165,7 @@
     silu_part = lax.dynamic_slice_in_dim(silu_low, feature_start, shard_rows, 1)
     mod_full, project_full = (
         lax.all_gather(modulation_weight, "dev", axis=0, tiled=True),
-        lax.all_gather(project_weight, "dev", axis=0, tiled=True),
+        touch_tokens(project_weight),
     )
     mod_table = jnp.einsum(
         "sd,jdc->sjc",

time: 4190 us -> 5040 us (1.20)
  waiting for transfers between devices: 2590 us -> 3330 us
  starting transfers between devices: 366 us -> 430 us
  blocking collectives: 145 us -> 91.7 us
  local copies, waits for them, and re-layouts: 237 us -> 290 us
    ppermute x0 -> x5, waiting for transfers between devices: none -> 1150 us  [wait_racks_all(): ppermute(back, 'dev', list(map(lambda i0: (i0, (i0 - r_now) % field_out),...]
    all_gather x1, waiting for transfers between devices: 307 us -> 0.01 us  [on_device(): lax.all_gather(modulation_weight, 'dev', axis=0, tiled=True)]
    all_gather x1, waiting for transfers between devices: 143 us -> 0.01 us  [on_device(): project_again = lax.all_gather(project_weight, 'dev', axis=0, tiled=True)]
    ppermute x72, starting transfers between devices: 365 us -> 423 us  [passed_along(): return lax.ppermute(x, axis, pairs)]
    psum x1, blocking collectives: 105 us -> 52.7 us  [on_device(): lax.psum(local_table.reshape(seq_count, 2, 6 * width), 'dev')]
  transfers between devices with their start and end apart: 79 -> 84, of which waited for: 31 -> 30; matrix products, arithmetic and copies ran while one was open for 11% -> 21% of each run, Pallas kernels for 0% -> 0%
where the time goes in v1:
time: 5040 us; the launch traced here: 5020 us
  waiting for transfers between devices  3330 us (66%)
  matrix products  628 us (12%)
  starting transfers between devices  430 us (9%)
  local copies, waits for them, and re-layouts  290 us (6%)
  other arithmetic  160 us (3%)
  blocking collectives  91.7 us (2%)
  loops' own time  76.6 us (2%)
    ppermute x5, waiting for transfers between devices, wait_racks_all(): ppermute(back, 'dev', list(map(lambda i0: (i0, (i0 - r_now) % field_out),...  1150 us
    reduce_scatter x1, waiting for transfers between devices, on_device(): lax.psum_scatter(jnp.concatenate([term_rows(attended_split, grad_merged),...  1090 us
    reduce_scatter x1, waiting for transfers between devices, on_device(): lax.psum_scatter(term_rows(activated_split, grad_lowered), 'dev', scatter...  656 us
    ppermute x72, waiting for transfers between devices, passed_along(): return lax.ppermute(x, axis, pairs)  428 us
    ppermute x72, starting transfers between devices, passed_along(): return lax.ppermute(x, axis, pairs)  423 us
  transfers between devices with their start and end apart: 84, of which 30 were waited for; matrix products, arithmetic and copies ran while one was open for 21% of the time, Pallas kernels for 0%

profile of v1, /device:TPU:0, one launch (start us, length us, event | category | flops | bytes accessed | tf_op | source)
XLA Modules:
  0.0 5018.3 jit_solution(15408323663334059411)
XLA Ops:
  16.4 16.1 collective-permute-done
  34.0 67.6 %collective-permute-done.1 = bf16[192,4608]{1,0:T(8,128)(2,1)S(1)} collective-permute-done((bf16[192,4608]{1,0:T(8,128)(2,1)S(1)}, bf16[192,4608]{1,0:T(8,128)(2,1)S(1)}, u32[]{:S(2)}, u32[]{:S(2)}) %collective-permute-start.1) | collective-permute-done | bytes 1769504 | tf_op jit(solution)/shard_map/ppermute | solution.py:28
  101.8 152.5 %collective-permute-done.2 = bf16[384,4608]{1,0:T(8,128)(2,1)S(1)} collective-permute-done((bf16[384,4608]{1,0:T(8,128)(2,1)S(1)}, bf16[384,4608]{1,0:T(8,128)(2,1)S(1)}, u32[]{:S(2)}, u32[]{:S(2)}) %collective-permute-start.2) | collective-permute-done | bytes 3538976 | tf_op jit(solution)/shard_map/ppermute | solution.py:28
  261.2 300.6 %collective-permute-done.3 = bf16[768,4608]{1,0:T(8,128)(2,1)} collective-permute-done((bf16[768,4608]{1,0:T(8,128)(2,1)S(1)}, bf16[768,4608]{1,0:T(8,128)(2,1)}, u32[]{:S(2)}, u32[]{:S(2)}) %collective-permute-start.3) | collective-permute-done | bytes 7077920 | tf_op jit(solution)/shard_map/ppermute | solution.py:28
  575.9 611.1 %collective-permute-done.4 = bf16[1536,4608]{1,0:T(8,128)(2,1)} collective-permute-done((bf16[1536,4608]{1,0:T(8,128)(2,1)}, bf16[1536,4608]{1,0:T(8,128)(2,1)}, u32[]{:S(2)}, u32[]{:S(2)}) %collective-permute-start.4) | collective-permute-done | bytes 14155808 | tf_op jit(solution)/shard_map/ppermute | solution.py:28
  1187.0 10.6 constant_dynamic-update-slice_fusion.11
  1209.4 11.1 constant_dynamic-update-slice_fusion.5
  1220.5 20.7 fusion.173
  1248.5 10.6 fusion.55
  1293.3 17.0 collective-permute-start.27
  1325.1 19.6 collective-permute-start.30
  1346.2 33.3 collective-permute-start.6
  1379.5 29.3 collective-permute-start.7
  1425.2 20.6 collective-permute-start.10
  1454.1 21.1 collective-permute-start.12
  1480.7 14.5 collective-permute-done.12
  1499.4 20.6 collective-permute-done.15
  1532.6 48.4 collective-permute-done.19
  1582.3 25.5 collective-permute-done.20
  1609.2 45.7 collective-permute-done.21
  1679.4 49.5 collective-permute-done.38
  1728.9 76.4 %collective-permute-done.39 = bf16[144,1536]{1,0:T(8,128)(2,1)S(1)} collective-permute-done((bf16[144,1536]{1,0:T(8,128)(2,1)S(1)}, bf16[144,1536]{1,0:T(8,128)(2,1)S(1)}, u32[]{:S(2)}, u32[]{:S(2)}) %collective-permute-start.39) | collective-permute-done | bytes 442400 | tf_op jit(solution)/shard_map/ppermute | solution.py:46
  1816.0 163.7 %while.28 = (s32[]{:T(128)}, bf16[24,144,64]{1,2,0:T(8,128)(2,1)S(1)}, f32[24,144]{1,0:T(8,128)}, s32[24]{0:T(128)S(1)}, bf16[144,1536]{1,0:T(8,128)(2,1)S(1)}, ...) while((s32[]{:T(128)}, ...), condition=%wide.region_12.13_spmd.clone, body=%wide.region_9.12_spmd.clone.sunk | while | flops 104799600 | bytes 6301395 | solution.py:217
  2012.5 10.2 fusion.39
  2026.2 16.2 broadcast_select_fusion.1
  2042.4 12.9 fusion.79
  2058.1 14.3 fusion.47
  2078.6 11.5 fusion.41
  2093.5 14.4 fusion.195
  2108.0 10.9 multiply_convert_fusion.2
  2132.3 345.8 %while.29 = (s32[]{:T(128)}, bf16[24,144,64]{1,2,0:T(8,128)(2,1)}, f32[24,2736,64]{1,2,0:T(8,128)}, f32[24,2736,64]{1,2,0:T(8,128)}, s32[24]{0:T(128)S(1)}, /*in...) while((s32[]{:T(128)}, bf16[24,144,64]{1,2,0:T(8,128)(2,1)}, ...), condition=%wide.region_19.20_spmd.clone, body=%wide.region_17.19_spmd.clone.sunk | while | flops 256667760 | bytes 15595029 | solution.py:277
  2496.2 82.1 %collective-permute-start.76 = (bf16[144,1536]{1,0:T(8,128)(2,1)}, bf16[144,1536]{1,0:T(8,128)(2,1)}, u32[]{:S(2)}, u32[]{:S(2)}) collective-permute-start(bf16[144,1536]{1,0:T(8,128)(2,1)} %copy.230), channel_id=1, source_target_pairs={{0,9},{1,10},{2,11},{3,12},{4,13},{5,14},{6,15},{7,16},{8,17},{9,1... | collective-permute-start | bytes 1327112 | tf_op jit(solution)/shard_map/ppermute | solution.py:46
  2580.5 33.7 collective-permute-start.75
  2616.3 16.4 collective-permute-start.74
  2694.7 13.1 fusion.202
  2726.3 21.3 collective-permute-done.64
  2795.7 28.1 fusion.133
  2879.7 19.2 collective-permute-done.46
  2904.5 47.1 collective-permute-done.42
  2956.2 21.8 fusion.137
  2978.0 97.8 %pad_maximum_fusion = f32[3072,12288]{1,0:T(8,128)} fusion(f32[3072,4608]{1,0:T(8,128)} %fusion.137, f32[3072,6144]{1,0:T(8,128)} %fusion.133, f32[3072,1536]{1,0:T(8,128)} %fusion.129), kind=kLoop, calls=%fused_computation.61 | loop fusion | flops 75497472 | bytes 301989888 | tf_op jit(solution)/shard_map/concatenate | solution.py:306
  3078.7 40.2 fusion.80
  3123.1 10.1 fusion.53
  3134.5 11.8 fusion.196
  3159.5 52.7 %all-reduce.2 = bf16[4,2,9216]{2,0,1:T(4,128)(2,1)S(1)} all-reduce(f32[4,2,9216]{2,0,1:T(4,128)S(1)} %copy.187), channel_id=1, replica_groups=mesh['dev'=32] {'dev'}, use_global_device_ids=true, to_apply=%region_22.23 | all-reduce | flops 73728 | bytes 442368 | tf_op jit(solution)/shard_map/psum | solution.py:333
  3212.7 39.0 all-gather
  3255.1 1092.1 %reduce-scatter.3.cloned.1.call-done = f32[96,12288]{1,0:T(8,128)} async-done(((f32[3072,12288]{1,0:T(8,128)}), f32[96,12288]{1,0:T(8,128)}) %reduce-scatter.3.cloned.1.call-update) | async-done | bytes 4718608 | tf_op jit(solution)/shard_map/reduce_scatter | solution.py:305
  4355.1 655.9 %reduce-scatter.5.cloned.1.call-done = f32[384,1536]{1,0:T(8,128)} async-done(((f32[12288,1536]{1,0:T(8,128)}), f32[384,1536]{1,0:T(8,128)}) %reduce-scatter.5.cloned.1.call-update) | async-done | bytes 2359312 | tf_op jit(solution)/shard_map/reduce_scatter | solution.py:234
  (838 shorter events, 929.7 us)
Async XLA Ops:
  7.2 1213.3 %all-gather.7.cloned.1.call-start = ((), (), s32[]{:S(2)}) async-start(), calls=%async_computation.2 | async-start | bytes 58392576 | tf_op jit(solution)/shard_map/all_gather | solution.py:167
  7.9 1974.3 %all-gather.9.cloned.1.call-start = ((), (), s32[]{:S(2)}) async-start(), calls=%async_computation.3 | async-start | bytes 9732096 | tf_op jit(solution)/shard_map/all_gather | solution.py:105
  8.7 1989.0 %all-gather.11.cloned.1.call-start = ((), (), s32[]{:S(2)}) async-start(), calls=%async_computation.4 | async-start | bytes 38928384 | tf_op jit(solution)/shard_map/all_gather | solution.py:106
  9.4 2003.1 %all-gather.13.cloned.1.call-start = ((), (), s32[]{:S(2)}) async-start(), calls=%async_computation.5 | async-start | bytes 38928384 | tf_op jit(solution)/shard_map/all_gather | solution.py:107
  10.0 3113.1 %all-gather.15.cloned.1.call-start = ((), (), s32[]{:S(2)}) async-start(), calls=%async_computation.6 | async-start | bytes 29196288 | tf_op jit(solution)/shard_map/all_gather | solution.py:302
  33.9 67.6 %collective-permute-start.1 = (bf16[192,4608]{1,0:T(8,128)(2,1)S(1)}, bf16[192,4608]{1,0:T(8,128)(2,1)S(1)}, u32[]{:S(2)}, u32[]{:S(2)}) collective-permute-start(bf16[192,4608]{1,0:T(8,128)(2,1)S(1)} %pad_maximum_fusion.3), channel_id=1, source_target_pairs={{0,30},{1,31},{2,0},{3,1},{4,2},{5,3},{6,4},{7,5},{8,6},{9,7},{10,... | collective-permute-start | bytes 5308424 | tf_op jit(solution)/shard_map/ppermute | solution.py:28
  101.8 152.6 %collective-permute-start.2 = (bf16[384,4608]{1,0:T(8,128)(2,1)S(1)}, bf16[384,4608]{1,0:T(8,128)(2,1)S(1)}, u32[]{:S(2)}, u32[]{:S(2)}) collective-permute-start(bf16[384,4608]{1,0:T(8,128)(2,1)S(1)} %pad_maximum_fusion.2), channel_id=1, source_target_pairs={{0,28},{1,29},{2,30},{3,31},{4,0},{5,1},{6,2},{7,3},{8,4},{9,5},{1... | collective-permute-start | bytes 10616840 | tf_op jit(solution)/shard_map/ppermute | solution.py:28
  255.0 306.8 %collective-permute-start.3 = (bf16[768,4608]{1,0:T(8,128)(2,1)S(1)}, bf16[768,4608]{1,0:T(8,128)(2,1)}, u32[]{:S(2)}, u32[]{:S(2)}) collective-permute-start(bf16[768,4608]{1,0:T(8,128)(2,1)S(1)} %pad_maximum_fusion.1), channel_id=1, source_target_pairs={{0,24},{1,25},{2,26},{3,27},{4,28},{5,29},{6,30},{7,31},{8,0},{9,1... | collective-permute-start | bytes 21233672 | tf_op jit(solution)/shard_map/ppermute | solution.py:28
  570.8 616.2 %collective-permute-start.4 = (bf16[1536,4608]{1,0:T(8,128)(2,1)}, bf16[1536,4608]{1,0:T(8,128)(2,1)}, u32[]{:S(2)}, u32[]{:S(2)}) collective-permute-start(bf16[1536,4608]{1,0:T(8,128)(2,1)} %get-tuple-element.275), channel_id=1, source_target_pairs={{0,16},{1,17},{2,18},{3,19},{4,20},{5,21},{6,22},{7,23},{8,24},{9,... | collective-permute-start | bytes 42467336 | tf_op jit(solution)/shard_map/ppermute | solution.py:28
  570.8 3776.3 %reduce-scatter.3.cloned.1.call-start = ((), (), s32[]{:S(2)}) async-start(), calls=%async_computation.7 | async-start | bytes 155713536 | tf_op jit(solution)/shard_map/reduce_scatter | solution.py:305
  1278.6 43.3 collective-permute-start.24
  1282.5 42.6 collective-permute-start.25
  1284.1 60.6 %collective-permute-start.26 = (bf16[144,1536]{1,0:T(8,128)(2,1)S(1)}, bf16[144,1536]{1,0:T(8,128)(2,1)S(1)}, u32[]{:S(2)}, u32[]{:S(2)}) collective-permute-start(bf16[144,1536]{1,0:T(8,128)(2,1)S(1)} %get-tuple-element.288), channel_id=1, source_target_pairs={{0,6},{1,7},{2,8},{3,9},{4,10},{5,11},{6,12},{7,13},{8,14},{9,15},... | collective-permute-start | bytes 1327112 | tf_op jit(solution)/shard_map/ppermute | solution.py:46
  1293.3 52.8 %collective-permute-start.27 = (bf16[144,1536]{1,0:T(8,128)(2,1)S(1)}, bf16[144,1536]{1,0:T(8,128)(2,1)S(1)}, u32[]{:S(2)}, u32[]{:S(2)}) collective-permute-start(bf16[144,1536]{1,0:T(8,128)(2,1)S(1)} %get-tuple-element.288), channel_id=1, source_target_pairs={{0,5},{1,6},{2,7},{3,8},{4,9},{5,10},{6,11},{7,12},{8,13},{9,14},{... | collective-permute-start | bytes 1327112 | tf_op jit(solution)/shard_map/ppermute | solution.py:46
  1310.4 69.2 %collective-permute-start.28 = (bf16[144,1536]{1,0:T(8,128)(2,1)S(1)}, bf16[144,1536]{1,0:T(8,128)(2,1)S(1)}, u32[]{:S(2)}, u32[]{:S(2)}) collective-permute-start(bf16[144,1536]{1,0:T(8,128)(2,1)S(1)} %get-tuple-element.288), channel_id=1, source_target_pairs={{0,4},{1,5},{2,6},{3,7},{4,8},{5,9},{6,10},{7,11},{8,12},{9,13},{1... | collective-permute-start | bytes 1327112 | tf_op jit(solution)/shard_map/ppermute | solution.py:46
  1321.9 87.0 %collective-permute-start.29 = (bf16[144,1536]{1,0:T(8,128)(2,1)S(1)}, bf16[144,1536]{1,0:T(8,128)(2,1)S(1)}, u32[]{:S(2)}, u32[]{:S(2)}) collective-permute-start(bf16[144,1536]{1,0:T(8,128)(2,1)S(1)} %get-tuple-element.288), channel_id=1, source_target_pairs={{0,3},{1,4},{2,5},{3,6},{4,7},{5,8},{6,9},{7,10},{8,11},{9,12},{10... | collective-permute-start | bytes 1327112 | tf_op jit(solution)/shard_map/ppermute | solution.py:46
  1325.1 92.2 %collective-permute-start.30 = (bf16[144,1536]{1,0:T(8,128)(2,1)S(1)}, bf16[144,1536]{1,0:T(8,128)(2,1)S(1)}, u32[]{:S(2)}, u32[]{:S(2)}) collective-permute-start(bf16[144,1536]{1,0:T(8,128)(2,1)S(1)} %get-tuple-element.288), channel_id=1, source_target_pairs={{0,2},{1,3},{2,4},{3,5},{4,6},{5,7},{6,8},{7,9},{8,10},{9,11},{10,... | collective-permute-start | bytes 1327112 | tf_op jit(solution)/shard_map/ppermute | solution.py:46
  1344.7 80.4 %collective-permute-start.31 = (bf16[144,1536]{1,0:T(8,128)(2,1)S(1)}, bf16[144,1536]{1,0:T(8,128)(2,1)S(1)}, u32[]{:S(2)}, u32[]{:S(2)}) collective-permute-start(bf16[144,1536]{1,0:T(8,128)(2,1)S(1)} %get-tuple-element.288), channel_id=1, source_target_pairs={{0,1},{1,2},{2,3},{3,4},{4,5},{5,6},{6,7},{7,8},{8,9},{9,10},{10,1... | collective-permute-start | bytes 1327112 | tf_op jit(solution)/shard_map/ppermute | solution.py:46
  1346.2 99.7 %collective-permute-start.6 = (bf16[144,1536]{1,0:T(8,128)(2,1)S(1)}, bf16[144,1536]{1,0:T(8,128)(2,1)S(1)}, u32[]{:S(2)}, u32[]{:S(2)}) collective-permute-start(bf16[144,1536]{1,0:T(8,128)(2,1)S(1)} %get-tuple-element.289), channel_id=1, source_target_pairs={{0,8},{1,9},{2,10},{3,11},{4,12},{5,13},{6,14},{7,15},{8,16},{9,17... | collective-permute-start | bytes 1327112 | tf_op jit(solution)/shard_map/ppermute | solution.py:46
  1379.5 74.6 %collective-permute-start.7 = (bf16[144,1536]{1,0:T(8,128)(2,1)S(1)}, bf16[144,1536]{1,0:T(8,128)(2,1)S(1)}, u32[]{:S(2)}, u32[]{:S(2)}) collective-permute-start(bf16[144,1536]{1,0:T(8,128)(2,1)S(1)} %get-tuple-element.289), channel_id=1, source_target_pairs={{0,7},{1,8},{2,9},{3,10},{4,11},{5,12},{6,13},{7,14},{8,15},{9,16}... | collective-permute-start | bytes 1327112 | tf_op jit(solution)/shard_map/ppermute | solution.py:46
  1408.9 66.4 %collective-permute-start.8 = (bf16[144,1536]{1,0:T(8,128)(2,1)S(1)}, bf16[144,1536]{1,0:T(8,128)(2,1)S(1)}, u32[]{:S(2)}, u32[]{:S(2)}) collective-permute-start(bf16[144,1536]{1,0:T(8,128)(2,1)S(1)} %get-tuple-element.289), channel_id=1, source_target_pairs={{0,6},{1,7},{2,8},{3,9},{4,10},{5,11},{6,12},{7,13},{8,14},{9,15},... | collective-permute-start | bytes 1327112 | tf_op jit(solution)/shard_map/ppermute | solution.py:46
  1417.3 59.4 %collective-permute-start.9 = (bf16[144,1536]{1,0:T(8,128)(2,1)S(1)}, bf16[144,1536]{1,0:T(8,128)(2,1)S(1)}, u32[]{:S(2)}, u32[]{:S(2)}) collective-permute-start(bf16[144,1536]{1,0:T(8,128)(2,1)S(1)} %get-tuple-element.289), channel_id=1, source_target_pairs={{0,5},{1,6},{2,7},{3,8},{4,9},{5,10},{6,11},{7,12},{8,13},{9,14},{... | collective-permute-start | bytes 1327112 | tf_op jit(solution)/shard_map/ppermute | solution.py:46
  1425.2 52.9 %collective-permute-start.10 = (bf16[144,1536]{1,0:T(8,128)(2,1)S(1)}, bf16[144,1536]{1,0:T(8,128)(2,1)S(1)}, u32[]{:S(2)}, u32[]{:S(2)}) collective-permute-start(bf16[144,1536]{1,0:T(8,128)(2,1)S(1)} %get-tuple-element.289), channel_id=1, source_target_pairs={{0,4},{1,5},{2,6},{3,7},{4,8},{5,9},{6,10},{7,11},{8,12},{9,13},{1... | collective-permute-start | bytes 1327112 | tf_op jit(solution)/shard_map/ppermute | solution.py:46
  1498.0 83.0 %collective-permute-start.19 = (bf16[144,1536]{1,0:T(8,128)(2,1)S(1)}, bf16[144,1536]{1,0:T(8,128)(2,1)S(1)}, u32[]{:S(2)}, u32[]{:S(2)}) collective-permute-start(bf16[144,1536]{1,0:T(8,128)(2,1)S(1)} %get-tuple-element.289), channel_id=1, source_target_pairs={{6,0},{7,1},{8,2},{9,3},{10,4},{11,5},{12,6},{13,7},{14,8},{15,9},... | collective-permute-start | bytes 1327112 | tf_op jit(solution)/shard_map/ppermute | solution.py:46
  1520.0 87.8 %collective-permute-start.20 = (bf16[144,1536]{1,0:T(8,128)(2,1)S(1)}, bf16[144,1536]{1,0:T(8,128)(2,1)S(1)}, u32[]{:S(2)}, u32[]{:S(2)}) collective-permute-start(bf16[144,1536]{1,0:T(8,128)(2,1)S(1)} %get-tuple-element.289), channel_id=1, source_target_pairs={{7,0},{8,1},{9,2},{10,3},{11,4},{12,5},{13,6},{14,7},{15,8},{16,9}... | collective-permute-start | bytes 1327112 | tf_op jit(solution)/shard_map/ppermute | solution.py:46
  1521.6 133.3 %collective-permute-start.21 = (bf16[144,1536]{1,0:T(8,128)(2,1)S(1)}, bf16[144,1536]{1,0:T(8,128)(2,1)S(1)}, u32[]{:S(2)}, u32[]{:S(2)}) collective-permute-start(bf16[144,1536]{1,0:T(8,128)(2,1)S(1)} %get-tuple-element.289), channel_id=1, source_target_pairs={{8,0},{9,1},{10,2},{11,3},{12,4},{13,5},{14,6},{15,7},{16,8},{17,9... | collective-permute-start | bytes 1327112 | tf_op jit(solution)/shard_map/ppermute | solution.py:46
  1522.9 136.7 %collective-permute-start.22 = (bf16[144,1536]{1,0:T(8,128)(2,1)S(1)}, bf16[144,1536]{1,0:T(8,128)(2,1)S(1)}, u32[]{:S(2)}, u32[]{:S(2)}) collective-permute-start(bf16[144,1536]{1,0:T(8,128)(2,1)S(1)} %get-tuple-element.289), channel_id=1, source_target_pairs={{9,0},{10,1},{11,2},{12,3},{13,4},{14,5},{15,6},{16,7},{17,8},{18,... | collective-permute-start | bytes 1327112 | tf_op jit(solution)/shard_map/ppermute | solution.py:46
  1531.3 129.7 %collective-permute-start.32 = (bf16[144,1536]{1,0:T(8,128)(2,1)S(1)}, bf16[144,1536]{1,0:T(8,128)(2,1)S(1)}, u32[]{:S(2)}, u32[]{:S(2)}) collective-permute-start(bf16[144,1536]{1,0:T(8,128)(2,1)S(1)} %get-tuple-element.288), channel_id=1, source_target_pairs={{1,0},{2,1},{3,2},{4,3},{5,4},{6,5},{7,6},{8,7},{9,8},{10,9},{11,1... | collective-permute-start | bytes 1327112 | tf_op jit(solution)/shard_map/ppermute | solution.py:46
  1581.0 81.3 %collective-permute-start.33 = (bf16[144,1536]{1,0:T(8,128)(2,1)S(1)}, bf16[144,1536]{1,0:T(8,128)(2,1)S(1)}, u32[]{:S(2)}, u32[]{:S(2)}) collective-permute-start(bf16[144,1536]{1,0:T(8,128)(2,1)S(1)} %get-tuple-element.288), channel_id=1, source_target_pairs={{2,0},{3,1},{4,2},{5,3},{6,4},{7,5},{8,6},{9,7},{10,8},{11,9},{12,... | collective-permute-start | bytes 1327112 | tf_op jit(solution)/shard_map/ppermute | solution.py:46
  1607.8 55.8 %collective-permute-start.34 = (bf16[144,1536]{1,0:T(8,128)(2,1)S(1)}, bf16[144,1536]{1,0:T(8,128)(2,1)S(1)}, u32[]{:S(2)}, u32[]{:S(2)}) collective-permute-start(bf16[144,1536]{1,0:T(8,128)(2,1)S(1)} %get-tuple-element.288), channel_id=1, source_target_pairs={{3,0},{4,1},{5,2},{6,3},{7,4},{8,5},{9,6},{10,7},{11,8},{12,9},{13... | collective-permute-start | bytes 1327112 | tf_op jit(solution)/shard_map/ppermute | solution.py:46
  1662.3 66.6 %collective-permute-start.38 = (bf16[144,1536]{1,0:T(8,128)(2,1)S(1)}, bf16[144,1536]{1,0:T(8,128)(2,1)S(1)}, u32[]{:S(2)}, u32[]{:S(2)}) collective-permute-start(bf16[144,1536]{1,0:T(8,128)(2,1)S(1)} %get-tuple-element.288), channel_id=1, source_target_pairs={{7,0},{8,1},{9,2},{10,3},{11,4},{12,5},{13,6},{14,7},{15,8},{16,9}... | collective-permute-start | bytes 1327112 | tf_op jit(solution)/shard_map/ppermute | solution.py:46
  1663.7 141.6 %collective-permute-start.39 = (bf16[144,1536]{1,0:T(8,128)(2,1)S(1)}, bf16[144,1536]{1,0:T(8,128)(2,1)S(1)}, u32[]{:S(2)}, u32[]{:S(2)}) collective-permute-start(bf16[144,1536]{1,0:T(8,128)(2,1)S(1)} %get-tuple-element.288), channel_id=1, source_target_pairs={{8,0},{9,1},{10,2},{11,3},{12,4},{13,5},{14,6},{15,7},{16,8},{17,9... | collective-permute-start | bytes 1327112 | tf_op jit(solution)/shard_map/ppermute | solution.py:46
  1675.1 137.6 %collective-permute-start.40 = (bf16[144,1536]{1,0:T(8,128)(2,1)S(1)}, bf16[144,1536]{1,0:T(8,128)(2,1)S(1)}, u32[]{:S(2)}, u32[]{:S(2)}) collective-permute-start(bf16[144,1536]{1,0:T(8,128)(2,1)S(1)} %get-tuple-element.288), channel_id=1, source_target_pairs={{9,0},{10,1},{11,2},{12,3},{13,4},{14,5},{15,6},{16,7},{17,8},{18,... | collective-permute-start | bytes 1327112 | tf_op jit(solution)/shard_map/ppermute | solution.py:46
  2496.2 147.1 %collective-permute-start.76 = (bf16[144,1536]{1,0:T(8,128)(2,1)}, bf16[144,1536]{1,0:T(8,128)(2,1)}, u32[]{:S(2)}, u32[]{:S(2)}) collective-permute-start(bf16[144,1536]{1,0:T(8,128)(2,1)} %copy.230), channel_id=1, source_target_pairs={{0,9},{1,10},{2,11},{3,12},{4,13},{5,14},{6,15},{7,16},{8,17},{9,1... | collective-permute-start | bytes 1327112 | tf_op jit(solution)/shard_map/ppermute | solution.py:46
  2580.5 75.8 %collective-permute-start.75 = (bf16[144,1536]{1,0:T(8,128)(2,1)}, bf16[144,1536]{1,0:T(8,128)(2,1)}, u32[]{:S(2)}, u32[]{:S(2)}) collective-permute-start(bf16[144,1536]{1,0:T(8,128)(2,1)} %copy.229), channel_id=1, source_target_pairs={{0,8},{1,9},{2,10},{3,11},{4,12},{5,13},{6,14},{7,15},{8,16},{9,17... | collective-permute-start | bytes 1327112 | tf_op jit(solution)/shard_map/ppermute | solution.py:46
  2689.4 58.2 %collective-permute-start.64 = (bf16[144,1536]{1,0:T(8,128)(2,1)}, bf16[144,1536]{1,0:T(8,128)(2,1)}, u32[]{:S(2)}, u32[]{:S(2)}) collective-permute-start(bf16[144,1536]{1,0:T(8,128)(2,1)} %copy.218), channel_id=1, source_target_pairs={{4,0},{5,1},{6,2},{7,3},{8,4},{9,5},{10,6},{11,7},{12,8},{13,9},{1... | collective-permute-start | bytes 1327112 | tf_op jit(solution)/shard_map/ppermute | solution.py:46
  2690.7 58.3 %collective-permute-start.63 = (bf16[144,1536]{1,0:T(8,128)(2,1)}, bf16[144,1536]{1,0:T(8,128)(2,1)}, u32[]{:S(2)}, u32[]{:S(2)}) collective-permute-start(bf16[144,1536]{1,0:T(8,128)(2,1)} %copy.217), channel_id=1, source_target_pairs={{5,0},{6,1},{7,2},{8,3},{9,4},{10,5},{11,6},{12,7},{13,8},{14,9},{... | collective-permute-start | bytes 1327112 | tf_op jit(solution)/shard_map/ppermute | solution.py:46
  2692.0 63.6 %collective-permute-start.62 = (bf16[144,1536]{1,0:T(8,128)(2,1)}, bf16[144,1536]{1,0:T(8,128)(2,1)}, u32[]{:S(2)}, u32[]{:S(2)}) collective-permute-start(bf16[144,1536]{1,0:T(8,128)(2,1)} %copy.216), channel_id=1, source_target_pairs={{6,0},{7,1},{8,2},{9,3},{10,4},{11,5},{12,6},{13,7},{14,8},{15,9},... | collective-permute-start | bytes 1327112 | tf_op jit(solution)/shard_map/ppermute | solution.py:46
  2693.4 68.4 %collective-permute-start.61 = (bf16[144,1536]{1,0:T(8,128)(2,1)}, bf16[144,1536]{1,0:T(8,128)(2,1)}, u32[]{:S(2)}, u32[]{:S(2)}) collective-permute-start(bf16[144,1536]{1,0:T(8,128)(2,1)} %copy.215), channel_id=1, source_target_pairs={{7,0},{8,1},{9,2},{10,3},{11,4},{12,5},{13,6},{14,7},{15,8},{16,9}... | collective-permute-start | bytes 1327112 | tf_op jit(solution)/shard_map/ppermute | solution.py:46
  2725.0 48.0 collective-permute-start.60
  2773.0 78.8 %collective-permute-start.55 = (bf16[144,1536]{1,0:T(8,128)(2,1)}, bf16[144,1536]{1,0:T(8,128)(2,1)}, u32[]{:S(2)}, u32[]{:S(2)}) collective-permute-start(bf16[144,1536]{1,0:T(8,128)(2,1)} %copy.208), channel_id=1, source_target_pairs={{0,6},{1,7},{2,8},{3,9},{4,10},{5,11},{6,12},{7,13},{8,14},{9,15},... | collective-permute-start | bytes 1327112 | tf_op jit(solution)/shard_map/ppermute | solution.py:46
  2779.6 73.6 %collective-permute-start.54 = (bf16[144,1536]{1,0:T(8,128)(2,1)}, bf16[144,1536]{1,0:T(8,128)(2,1)}, u32[]{:S(2)}, u32[]{:S(2)}) collective-permute-start(bf16[144,1536]{1,0:T(8,128)(2,1)} %copy.207), channel_id=1, source_target_pairs={{0,5},{1,6},{2,7},{3,8},{4,9},{5,10},{6,11},{7,12},{8,13},{9,14},{... | collective-permute-start | bytes 1327112 | tf_op jit(solution)/shard_map/ppermute | solution.py:46
  2781.7 72.9 %collective-permute-start.53 = (bf16[144,1536]{1,0:T(8,128)(2,1)}, bf16[144,1536]{1,0:T(8,128)(2,1)}, u32[]{:S(2)}, u32[]{:S(2)}) collective-permute-start(bf16[144,1536]{1,0:T(8,128)(2,1)} %copy.206), channel_id=1, source_target_pairs={{0,4},{1,5},{2,6},{3,7},{4,8},{5,9},{6,10},{7,11},{8,12},{9,13},{1... | collective-permute-start | bytes 1327112 | tf_op jit(solution)/shard_map/ppermute | solution.py:46
  2785.6 70.3 %collective-permute-start.52 = (bf16[144,1536]{1,0:T(8,128)(2,1)}, bf16[144,1536]{1,0:T(8,128)(2,1)}, u32[]{:S(2)}, u32[]{:S(2)}) collective-permute-start(bf16[144,1536]{1,0:T(8,128)(2,1)} %copy.205), channel_id=1, source_target_pairs={{0,3},{1,4},{2,5},{3,6},{4,7},{5,8},{6,9},{7,10},{8,11},{9,12},{10... | collective-permute-start | bytes 1327112 | tf_op jit(solution)/shard_map/ppermute | solution.py:46
  2793.2 64.0 %collective-permute-start.51 = (bf16[144,1536]{1,0:T(8,128)(2,1)}, bf16[144,1536]{1,0:T(8,128)(2,1)}, u32[]{:S(2)}, u32[]{:S(2)}) collective-permute-start(bf16[144,1536]{1,0:T(8,128)(2,1)} %copy.204), channel_id=1, source_target_pairs={{0,2},{1,3},{2,4},{3,5},{4,6},{5,7},{6,8},{7,9},{8,10},{9,11},{10,... | collective-permute-start | bytes 1327112 | tf_op jit(solution)/shard_map/ppermute | solution.py:46
  2878.4 73.2 %collective-permute-start.42 = (bf16[144,1536]{1,0:T(8,128)(2,1)S(1)}, bf16[144,1536]{1,0:T(8,128)(2,1)S(1)}, u32[]{:S(2)}, u32[]{:S(2)}) collective-permute-start(bf16[144,1536]{1,0:T(8,128)(2,1)S(1)} %copy-done.41), channel_id=1, source_target_pairs={{8,0},{9,1},{10,2},{11,3},{12,4},{13,5},{14,6},{15,7},{16,8},{17,9... | collective-permute-start | bytes 1327112 | tf_op jit(solution)/shard_map/ppermute | solution.py:46
  2898.9 54.3 %collective-permute-start.41 = (bf16[144,1536]{1,0:T(8,128)(2,1)S(1)}, bf16[144,1536]{1,0:T(8,128)(2,1)S(1)}, u32[]{:S(2)}, u32[]{:S(2)}) collective-permute-start(bf16[144,1536]{1,0:T(8,128)(2,1)S(1)} %copy-done.43), channel_id=1, source_target_pairs={{9,0},{10,1},{11,2},{12,3},{13,4},{14,5},{15,6},{16,7},{17,8},{18,... | collective-permute-start | bytes 1327112 | tf_op jit(solution)/shard_map/ppermute | solution.py:46
  3075.9 1935.1 %reduce-scatter.5.cloned.1.call-start = ((), (), s32[]{:S(2)}) async-start(), calls=%async_computation.8 | async-start | bytes 77856768 | tf_op jit(solution)/shard_map/reduce_scatter | solution.py:234
  (118 other events, 4519.4 us)
Sparse Core Ops, SparseCore 0:
  10.9 548.7 all-gather.6
  562.6 686.3 all-gather.8
  1251.9 308.6 all-gather.10
  1563.3 382.0 all-gather.12
  1948.1 165.7 all-gather.14
  3076.0 1271.0 reduce-scatter.2
  4355.3 655.6 reduce-scatter.4
